TPU v7x, 32 devices: a whole 2x2x4 slice. The times are simulated.
32 devices in a mesh: job: 2 (over y), aux: 16 (over z, x, core).
Axes of the slice: x: 2, y: 2, z: 4, core: 2. Of those that a mesh axis runs over, the one named last changes fastest.
Arguments:
- ints_ov: bfloat16 [256, 384, 384], P(('job', 'aux')), parts along dimension 0, may hold values from -0.3125 to 0.3125
- ints_oo: bfloat16 [256, 2, 384], P(('job', 'aux')), parts along dimension 0, may hold values from -1.5 to 1.5
- trial: bfloat16 [64, 4, 384], P('job'), parts along dimension 0, may hold values from -6 to 6
- occ_energy: float32 [64], P('job'), parts along dimension 0, may hold values from -1 to -0.2
- vir_energy: float32 [32000], P('job'), parts along dimension 0, may hold values from 0.2 to 2.5
- root_shift: float32 [8], P('job'), parts along dimension 0, may hold values from 0.1 to 0.6
- vir_blocks: int32 [32, 3], P('job'), parts along dimension 0, may hold values from 0 to 124, as said below
- pair_list: int32 [32, 4, 2], P('job'), parts along dimension 0, may hold values from 0 to 31, as said below
- pair_count: int32 [32], P('job'), parts along dimension 0, may hold values from 2 to 4, as said below
Outputs:
- sigma: float32 [64, 4, 384], P(('job', 'aux')), parts along dimension 0
There are 2 independent parts, one for each index of `job`. A program takes and returns all parts, laid end to end along the dimension named above; each array names one. Nothing has to cross between parts.
Inputs may be any that keep to these rules, and one draw needn't show every extreme that they name: `pair_count`: some domain has 4 live pairs. `pair_list`: for domain d all 4 slots hold distinct pairs (i, j): i an occupied of domain d (d * 2 to d * 2 + 1) and j an occupied of one of the domains d + 1 to d + 3, taken cyclically modulo 16; slots from pair_count[d] on are not live. `vir_blocks`: the blocks of one domain are distinct.
All inputs are finite; a program needn't handle non-finite values.
Results may differ from a plain program's by a relative error of at most 0.00036.
Values may be sent and summed in bfloat16 or wider, within the bound.
A program may use at most 128 MiB of HBM per device.

v0:
```python
import functools

import jax
import jax.numpy as jnp
from jax import lax
from jax.experimental import pallas as pl
from jax.experimental.pallas import tpu as pltpu
from jax.sharding import PartitionSpec as P

F32 = jnp.float32
BF16 = jnp.bfloat16
LANES = 128


def split_high_low(value):
    high = value.astype(BF16).astype(F32)
    return high, (value - high).astype(BF16).astype(F32)


def sigma_kernel(
    ndomain, span, slot_count, occ_domain, root_count,
    ints_hbm, couple_hbm, trial_hbm, level_hbm, occ_energy, root_shift, pair_count, vir_blocks, pairs,
    out_ref,
    ints, couple, trial, level_table, levels_col, blocks_own, pairs_own, stage, landed,
    ints_sem, small_sem, send_sem, recv_sem,
):
    me = lax.axis_index("aux")
    slab_rows, fitting, virt = ints.shape
    width_blocks = virt // LANES
    rows = occ_domain * root_count

    def ahead(steps):
        return lax.rem(me + steps, ndomain)

    barrier = pltpu.get_barrier_semaphore()
    for steps in range(1, span):
        for other in (ahead(steps), ahead(ndomain - steps)):
            pl.semaphore_signal(
                barrier, inc=1, device_id={"aux": other}, device_id_type=pl.DeviceIdType.MESH
            )

    small = [
        pltpu.make_async_copy(pairs.at[me], pairs_own, small_sem.at[0]),
        pltpu.make_async_copy(couple_hbm, couple, small_sem.at[1]),
        pltpu.make_async_copy(level_hbm, level_table, small_sem.at[2]),
    ]
    for steps in range(span):
        small.append(
            pltpu.make_async_copy(
                vir_blocks.at[ahead(steps)], blocks_own.at[steps], small_sem.at[3 + 2 * steps]
            )
        )
        small.append(
            pltpu.make_async_copy(
                trial_hbm.at[pl.ds(ahead(steps) * occ_domain, occ_domain)],
                trial.at[pl.ds(steps * occ_domain, occ_domain)],
                small_sem.at[4 + 2 * steps],
            )
        )
    for copy in small:
        copy.start()
    big = [pltpu.make_async_copy(ints_hbm.at[row], ints.at[row], ints_sem.at[row]) for row in range(slab_rows)]
    for copy in big:
        copy.start()
    for copy in small:
        copy.wait()

    def level_rows(relative):
        return [level_table[pl.ds(blocks_own[relative, block], 1), :] for block in range(width_blocks)]

    for block, row in enumerate(level_rows(0)):
        levels_col[pl.ds(block * LANES, LANES), :] = jnp.broadcast_to(row, (LANES, LANES)).T

    row_index = lax.broadcasted_iota(jnp.int32, (rows, 1), 0)

    def trial_rows(relative):
        return jnp.concatenate(
            [trial[relative * occ_domain + own].astype(F32) for own in range(occ_domain)], axis=0
        )

    def couple_rows(slab_row):
        values = couple[slab_row].astype(F32)
        result = jnp.broadcast_to(values[0:1], (rows, fitting))
        for own in range(1, occ_domain):
            result = jnp.where(row_index >= own * root_count, values[own : own + 1], result)
        return result.astype(BF16)

    for copy in big:
        copy.wait()

    trial_first = trial_rows(0)
    live_slots = pair_count[me]

    def visit(slot, totals):
        occ_first = pairs_own[slot, 0]
        occ_second = pairs_own[slot, 1]
        relative = jnp.minimum(lax.rem(occ_second // occ_domain - me + ndomain, ndomain), span - 1)
        row_first = lax.rem(occ_first, occ_domain)
        row_second = relative * occ_domain + lax.rem(occ_second, occ_domain)

        mixed_first = jnp.dot(couple_rows(row_second), ints[row_first], preferred_element_type=F32)
        mixed_second = jnp.dot(couple_rows(row_first), ints[row_second], preferred_element_type=F32)
        first_high, first_low = split_high_low(mixed_first)
        second_high, second_low = split_high_low(mixed_second)
        trial_second = trial_rows(relative)
        left = jnp.concatenate([trial_first, trial_first, first_high, first_low], axis=0).T.astype(BF16)
        right = jnp.concatenate([second_high, second_low, trial_second, trial_second], axis=0)
        right_root = lax.broadcasted_iota(jnp.int32, (4 * rows, 1), 0) % root_count
        first_pair = jnp.concatenate([first_high, first_low], axis=0).astype(BF16)
        level_row = jnp.concatenate(level_rows(relative), axis=1) - occ_energy[occ_first] - occ_energy[occ_second]
        level_col = jnp.concatenate([levels_col[...]] * width_blocks, axis=1)

        sum_first = jnp.zeros((2 * rows, virt), F32)
        sum_second = jnp.zeros((rows, virt), F32)
        for root in range(root_count):
            right_now = jnp.where(right_root == root, right, 0.0).astype(BF16)
            coupled = jnp.dot(left, right_now, preferred_element_type=F32)
            doubles = (coupled / (level_col + (level_row - root_shift[root]))).astype(BF16)
            sum_first += lax.dot_general(
                right_now[: 2 * rows], doubles, (((1,), (1,)), ((), ())), preferred_element_type=F32
            )
            part = jnp.dot(first_pair, doubles, preferred_element_type=F32)
            part = part[:rows] + part[rows:]
            sum_second += jnp.where(row_index % root_count == root, part, 0.0)
        live = live_slots > slot
        sum_first = jnp.where(live, sum_first[:rows] + sum_first[rows:], 0.0)
        new_totals = [totals[0] + sum_first]
        for steps in range(1, span):
            new_totals.append(
                totals[steps] + jnp.where(jnp.logical_and(live, relative == steps), sum_second, 0.0)
            )
        return tuple(new_totals)

    totals = tuple(jnp.zeros((rows, virt), F32) for _ in range(span))
    if UNROLL:
        for slot in range(slot_count):
            totals = visit(slot, totals)
    else:
        totals = lax.fori_loop(0, slot_count, visit, totals)

    for steps in range(1, span):
        stage[steps - 1] = totals[steps]
    pl.semaphore_wait(barrier, 2 * (span - 1))
    copies = []
    for steps in range(1, span):
        copy = pltpu.make_async_remote_copy(
            src_ref=stage.at[steps - 1],
            dst_ref=landed.at[steps - 1],
            send_sem=send_sem.at[steps - 1],
            recv_sem=recv_sem.at[steps - 1],
            device_id={"aux": ahead(steps)},
            device_id_type=pl.DeviceIdType.MESH,
        )
        copy.start()
        copies.append(copy)
    result = totals[0]
    for copy in copies:
        copy.wait()
    for steps in range(1, span):
        result = result + landed[steps - 1]
    for own in range(occ_domain):
        out_ref[own] = result[own * root_count : (own + 1) * root_count]


UNROLL = True


def per_device(
    ints_ov, ints_oo, trial, occ_energy, vir_energy, root_shift, vir_blocks, pair_list, pair_count
):
    slab_rows, fitting, virt = ints_ov.shape
    occ_domain = ints_oo.shape[1]
    root_count = trial.shape[1]
    slot_count = pair_list.shape[1]
    span = slab_rows // occ_domain
    rows = occ_domain * root_count
    level_table = vir_energy.reshape(-1, LANES)
    anywhere = pl.BlockSpec(memory_space=pl.ANY)
    scalars = pl.BlockSpec(memory_space=pltpu.SMEM)
    return pl.pallas_call(
        functools.partial(
            sigma_kernel, lax.axis_size("aux"), span, slot_count, occ_domain, root_count
        ),
        out_shape=jax.ShapeDtypeStruct((occ_domain, root_count, virt), F32),
        in_specs=[anywhere] * 4 + [scalars] * 3 + [anywhere] * 2,
        out_specs=pl.BlockSpec(memory_space=pltpu.VMEM),
        scratch_shapes=[
            pltpu.VMEM(ints_ov.shape, BF16),
            pltpu.VMEM(ints_oo.shape, BF16),
            pltpu.VMEM((span * occ_domain, root_count, virt), BF16),
            pltpu.VMEM(level_table.shape, F32),
            pltpu.VMEM((virt, LANES), F32),
            pltpu.SMEM((span, vir_blocks.shape[1]), jnp.int32),
            pltpu.SMEM(pair_list.shape[1:], jnp.int32),
            pltpu.VMEM((span - 1, rows, virt), F32),
            pltpu.VMEM((span - 1, rows, virt), F32),
            pltpu.SemaphoreType.DMA((slab_rows,)),
            pltpu.SemaphoreType.DMA((3 + 2 * span,)),
            pltpu.SemaphoreType.DMA((span - 1,)),
            pltpu.SemaphoreType.DMA((span - 1,)),
        ],
        compiler_params=pltpu.CompilerParams(collective_id=0, has_side_effects=True),
        name="sigma",
    )(
        ints_ov, ints_oo, trial, level_table, occ_energy, root_shift, pair_count, vir_blocks, pair_list
    )


def solution(mesh):
    in_specs = (
        P(("job", "aux"), None, None),
        P(("job", "aux"), None, None),
        P("job", None, None),
        P("job"),
        P("job"),
        P("job"),
        P("job", None),
        P("job", None, None),
        P("job"),
    )
    out_specs = P(("job", "aux"), None, None)
    return jax.shard_map(
        per_device, mesh=mesh, in_specs=in_specs, out_specs=out_specs, check_vma=False
    )
```

profile of v0, /device:TPU:0, one launch (start us, length us, event | category | flops | bytes accessed | tf_op | source)
XLA Modules:
  0.0 20.7 jit_solution(12486487254027797090)
XLA Ops:
  0.0 1.4 %copy.10.vir_blocks = s32[16,3]{1,0:T(8,128)} copy(s32[16,3]{0,1:T(4,128)} %param.15) | data formatting | bytes 384 | tf_op args[6]
  1.4 1.4 %copy.11.pairs = s32[16,4,2]{2,1,0:T(4,128)} copy(s32[16,4,2]{0,2,1:T(2,128)} %param.16) | data formatting | bytes 1024 | tf_op args[7]
  2.7 16.7 %sigma.1 = f32[2,4,384]{2,1,0:T(4,128)} custom-call(bf16[8,384,384]{2,1,0:T(8,128)(2,1)} %ints_hbm.1, bf16[8,2,384]{2,1,0:T(2,128)(2,1)} %couple_hbm.1, bf16[32,4,384]{2,1,0:T(4,128)(2,1)} %trial_hbm.1, f32[125,128]{1,0:T(8,128)} %bitcast.1, f32[32]{0:T(128)} %occ_energy.1, f32[4]{0:T(128)} %root_shift.1, s32[16]{0:T(128)} %pair_count.1, ...), custom_call_target="tpu_custom_call" | custom-call | tf_op jit(solution)/shard_map/sigma/pallas_call | solution.py:180
  19.4 1.3 %copy.13 = f32[2,4,384]{2,1,0:T(4,128)} copy(f32[2,4,384]{2,1,0:T(4,128)} %sigma.1) | data formatting | bytes 24576
where the time goes:
time: 21 us; the launch traced here: 20.7 us
  Pallas kernels  16.7 us (80%)
  local copies, waits for them, and re-layouts  4.04 us (19%)
    pallas_call x1, Pallas kernels, per_device(): pl.pallas_call(functools.partial(sigma_kernel, lax.axis_size('aux'), span...  16.7 us
    unnamed x3, local copies, waits for them, and re-layouts  4.04 us

commit v1 on v0

v1 whole, which is shorter than its diff:
```python
import functools

import jax
import jax.numpy as jnp
from jax import lax
from jax.experimental import pallas as pl
from jax.experimental.pallas import tpu as pltpu
from jax.sharding import PartitionSpec as P

F32 = jnp.float32
BF16 = jnp.bfloat16
LANES = 128


def split_high_low(value):
    high = value.astype(BF16).astype(F32)
    return high, (value - high).astype(BF16).astype(F32)


def sigma_kernel(
    ndomain, span, slot_count, occ_domain, root_count,
    ints_hbm, couple_hbm, trial_hbm, level_hbm, occ_energy, root_shift, pair_count, vir_blocks, pairs,
    out_ref,
    ints, couple, trial, level_table, levels_col, mixed_own, mixed_far, doubles, stage, landed,
    ints_sem, small_sem, send_sem, recv_sem,
):
    me = lax.axis_index("aux")
    slab_rows, fitting, virt = ints.shape
    width_blocks = virt // LANES
    rows = occ_domain * root_count

    def ahead(steps):
        return lax.rem(me + steps, ndomain)

    barrier = pltpu.get_barrier_semaphore()
    for steps in range(1, span):
        for other in (ahead(steps), ahead(ndomain - steps)):
            pl.semaphore_signal(
                barrier, inc=1, device_id={"aux": other}, device_id_type=pl.DeviceIdType.MESH
            )

    small = [
        pltpu.make_async_copy(couple_hbm, couple, small_sem.at[0]),
        pltpu.make_async_copy(level_hbm, level_table, small_sem.at[1]),
    ]
    for steps in range(span):
        small.append(
            pltpu.make_async_copy(
                trial_hbm.at[pl.ds(ahead(steps) * occ_domain, occ_domain)],
                trial.at[pl.ds(steps * occ_domain, occ_domain)],
                small_sem.at[2 + steps],
            )
        )
    for copy in small:
        copy.start()
    big = [pltpu.make_async_copy(ints_hbm.at[row], ints.at[row], ints_sem.at[row]) for row in range(slab_rows)]
    for copy in big:
        copy.start()
    for copy in small:
        copy.wait()

    def level_rows(relative):
        return [level_table[pl.ds(vir_blocks[block, ahead(relative)], 1), :] for block in range(width_blocks)]

    for block, row in enumerate(level_rows(0)):
        levels_col[pl.ds(block * LANES, LANES), :] = jnp.broadcast_to(row, (LANES, LANES)).T

    row_index = lax.broadcasted_iota(jnp.int32, (rows, 1), 0)

    def trial_rows(relative):
        return jnp.concatenate(
            [trial[relative * occ_domain + own].astype(F32) for own in range(occ_domain)], axis=0
        )

    def couple_rows(slab_row):
        values = couple[slab_row].astype(F32)
        result = jnp.broadcast_to(values[0:1], (rows, fitting))
        for own in range(1, occ_domain):
            result = jnp.where(row_index >= own * root_count, values[own : own + 1], result)
        return result.astype(BF16)

    couple_all = [couple_rows(row) for row in range(slab_rows)]
    own_couple = jnp.concatenate(couple_all[:occ_domain], axis=0)
    far_couple = jnp.concatenate(couple_all[occ_domain:], axis=0)
    far_rows = slab_rows - occ_domain
    for row in range(slab_rows):
        big[row].wait()
        if row < occ_domain:
            mixed = jnp.dot(far_couple, ints[row], preferred_element_type=F32)
            for far in range(far_rows):
                mixed_own[row * far_rows + far] = mixed[far * rows : (far + 1) * rows]
        else:
            mixed = jnp.dot(own_couple, ints[row], preferred_element_type=F32)
            for own in range(occ_domain):
                mixed_far[own * far_rows + row - occ_domain] = mixed[own * rows : (own + 1) * rows]

    trial_first = trial_rows(0)
    live_slots = pair_count[me]
    right_root = lax.broadcasted_iota(jnp.int32, (4 * rows, 1), 0) % root_count
    totals = [jnp.zeros((rows, virt), F32) for _ in range(span)]
    weights = []
    for slot in range(slot_count):
        occ_first = pairs[slot, 0, me]
        occ_second = pairs[slot, 1, me]
        relative = lax.rem(occ_second // occ_domain - me + ndomain, ndomain)
        relative = jnp.maximum(jnp.minimum(relative, span - 1), 1)
        own = lax.rem(occ_first, occ_domain)
        place = own * far_rows + (relative - 1) * occ_domain + lax.rem(occ_second, occ_domain)
        live = live_slots > slot

        first_high, first_low = split_high_low(mixed_own[place])
        second_high, second_low = split_high_low(mixed_far[place])
        trial_second = trial_rows(relative)
        left = jnp.concatenate([trial_first, trial_first, first_high, first_low], axis=0).T.astype(BF16)
        right = jnp.concatenate([second_high, second_low, trial_second, trial_second], axis=0)
        right = jnp.concatenate(
            [jnp.where(right_root == root, right, 0.0) for root in range(root_count)], axis=1
        ).astype(BF16)
        first_pair = jnp.concatenate([first_high, first_low], axis=0).astype(BF16)
        level_row = jnp.concatenate(level_rows(relative), axis=1) - occ_energy[occ_first] - occ_energy[occ_second]
        level_row = jnp.concatenate([level_row - root_shift[root] for root in range(root_count)], axis=1)
        level_col = jnp.concatenate([levels_col[...]] * (width_blocks * root_count), axis=1)

        coupled = jnp.dot(left, right, preferred_element_type=F32)
        answer = (coupled / (level_col + level_row)).astype(BF16)
        doubles[slot] = answer
        weights.append(right[: 2 * rows])
        part = jnp.dot(first_pair, answer, preferred_element_type=F32)
        part = part[:rows] + part[rows:]
        second = jnp.zeros((rows, virt), F32)
        for root in range(root_count):
            second += jnp.where(
                row_index % root_count == root, part[:, root * virt : (root + 1) * virt], 0.0
            )
        for steps in range(1, span):
            totals[steps] += jnp.where(jnp.logical_and(live, relative == steps), second, 0.0)

    for steps in range(1, span):
        stage[steps - 1] = totals[steps]
    pl.semaphore_wait(barrier, 2 * (span - 1))
    copies = []
    for steps in range(1, span):
        copy = pltpu.make_async_remote_copy(
            src_ref=stage.at[steps - 1],
            dst_ref=landed.at[steps - 1],
            send_sem=send_sem.at[steps - 1],
            recv_sem=recv_sem.at[steps - 1],
            device_id={"aux": ahead(steps)},
            device_id_type=pl.DeviceIdType.MESH,
        )
        copy.start()
        copies.append(copy)
    result = totals[0]
    for slot in range(slot_count):
        first = lax.dot_general(
            weights[slot], doubles[slot], (((1,), (1,)), ((), ())), preferred_element_type=F32
        )
        result += jnp.where(live_slots > slot, first[:rows] + first[rows:], 0.0)
    for copy in copies:
        copy.wait()
    for steps in range(1, span):
        result = result + landed[steps - 1]
    for own in range(occ_domain):
        out_ref[own] = result[own * root_count : (own + 1) * root_count]


def per_device(
    ints_ov, ints_oo, trial, occ_energy, vir_energy, root_shift, vir_blocks, pair_list, pair_count
):
    slab_rows, fitting, virt = ints_ov.shape
    occ_domain = ints_oo.shape[1]
    root_count = trial.shape[1]
    slot_count = pair_list.shape[1]
    span = slab_rows // occ_domain
    rows = occ_domain * root_count
    level_table = vir_energy.reshape(-1, LANES)
    anywhere = pl.BlockSpec(memory_space=pl.ANY)
    scalars = pl.BlockSpec(memory_space=pltpu.SMEM)
    return pl.pallas_call(
        functools.partial(
            sigma_kernel, lax.axis_size("aux"), span, slot_count, occ_domain, root_count
        ),
        out_shape=jax.ShapeDtypeStruct((occ_domain, root_count, virt), F32),
        in_specs=[anywhere] * 4 + [scalars] * 5,
        out_specs=pl.BlockSpec(memory_space=pltpu.VMEM),
        scratch_shapes=[
            pltpu.VMEM(ints_ov.shape, BF16),
            pltpu.VMEM(ints_oo.shape, BF16),
            pltpu.VMEM((span * occ_domain, root_count, virt), BF16),
            pltpu.VMEM(level_table.shape, F32),
            pltpu.VMEM((virt, LANES), F32),
            pltpu.VMEM((occ_domain * (slab_rows - occ_domain), rows, virt), F32),
            pltpu.VMEM((occ_domain * (slab_rows - occ_domain), rows, virt), F32),
            pltpu.VMEM((slot_count, virt, root_count * virt), BF16),
            pltpu.VMEM((span - 1, rows, virt), F32),
            pltpu.VMEM((span - 1, rows, virt), F32),
            pltpu.SemaphoreType.DMA((slab_rows,)),
            pltpu.SemaphoreType.DMA((2 + span,)),
            pltpu.SemaphoreType.DMA((span - 1,)),
            pltpu.SemaphoreType.DMA((span - 1,)),
        ],
        compiler_params=pltpu.CompilerParams(collective_id=0, has_side_effects=True),
        name="sigma",
    )(
        ints_ov, ints_oo, trial, level_table, occ_energy, root_shift, pair_count, vir_blocks.T,
        pair_list.transpose(1, 2, 0),
    )


def solution(mesh):
    in_specs = (
        P(("job", "aux"), None, None),
        P(("job", "aux"), None, None),
        P("job", None, None),
        P("job"),
        P("job"),
        P("job"),
        P("job", None),
        P("job", None, None),
        P("job"),
    )
    out_specs = P(("job", "aux"), None, None)
    return jax.shard_map(
        per_device, mesh=mesh, in_specs=in_specs, out_specs=out_specs, check_vma=False
    )
```

time: 21 us -> 16.9 us (0.80)
  local copies, waits for them, and re-layouts: 4.04 us -> 1.31 us
  Pallas kernels: 16.7 us -> 15.3 us
    unnamed x3 -> x1, local copies, waits for them, and re-layouts: 4.04 us -> 1.31 us
    pallas_call x1, Pallas kernels: 16.7 us -> 15.3 us  [per_device(): pl.pallas_call(functools.partial(sigma_kernel, lax.axis_size('aux'), span...]
where the time goes in v1:
time: 16.9 us; the launch traced here: 16.6 us
  Pallas kernels  15.3 us (91%)
  local copies, waits for them, and re-layouts  1.31 us (8%)
    pallas_call x1, Pallas kernels, per_device(): pl.pallas_call(functools.partial(sigma_kernel, lax.axis_size('aux'), span...  15.3 us
    unnamed x1, local copies, waits for them, and re-layouts  1.31 us

profile of v1, /device:TPU:0, one launch (start us, length us, event | category | flops | bytes accessed | tf_op | source)
XLA Modules:
  0.0 16.6 jit_solution(12785303498941207405)
XLA Ops:
  0.0 15.3 %sigma.1 = f32[2,4,384]{2,1,0:T(4,128)} custom-call(bf16[8,384,384]{2,1,0:T(8,128)(2,1)} %ints_hbm.1, bf16[8,2,384]{2,1,0:T(2,128)(2,1)} %couple_hbm.1, bf16[32,4,384]{2,1,0:T(4,128)(2,1)} %trial_hbm.1, f32[125,128]{1,0:T(8,128)} %bitcast.3, f32[32]{0:T(128)} %occ_energy.1, f32[4]{0:T(128)} %root_shift.1, s32[16]{0:T(128)} %pair_count.1, s32[3,16]{1,0:T(4,128)} %bitcast.5, ...), custom_call_target="tpu_custom_call" | custom-call | tf_op jit(solution)/shard_map/sigma/pallas_call | solution.py:179
  15.3 1.3 %copy.11 = f32[2,4,384]{2,1,0:T(4,128)} copy(f32[2,4,384]{2,1,0:T(4,128)} %sigma.1) | data formatting | bytes 24576
